TPU v7x, 32 devices: a whole 2x2x4 slice. The times are simulated.
32 devices in a mesh: tm: 2 (over core), stn: 4 (over z), chan: 4 (over y, x).
Axes of the slice: x: 2, y: 2, z: 4, core: 2. Of those that a mesh axis runs over, the one named last changes fastest.
Arguments:
- voltages: bfloat16 [2, 8, 512, 32, 2, 256], P(None, 'chan', 'stn', 'tm'), may hold values from -100 to 100
- fir_taps: float32 [16, 256], replicated, may hold values from -1.5 to 1.5
- station_map: int32 [512], P('stn'), may hold values from 0 to 31, as said below
- beam_index: int32 [512], P('stn'), may hold values from 0 to 15
- weight_table: bfloat16 [2, 16, 8, 8], P(None, None, 'chan'), may hold values from -1.5 to 1.5
Outputs:
- visibilities: float32 [2, 2, 8, 32, 32, 8, 2, 2, 256], P('tm', None, 'chan', 'stn')
Inputs may be any that keep to these rules, and one draw needn't show every extreme that they name: `station_map`: each station number names exactly 16 dishes; of the dishes g * 128 up to (g + 1) * 128 - 1, exactly 32 name a station of the block h * 8 up to (h + 1) * 8 - 1, for every g and h.
All inputs are finite; a program needn't handle non-finite values.
Results may differ from a plain program's by a relative error of at most 0.017.
Values may be sent and summed in bfloat16 or wider, within the bound.
A program may use at most 512 MiB of HBM per device.

v0:
```python
import jax
import jax.numpy as jnp
from jax import lax
from jax.sharding import PartitionSpec as P

STATIONS = 32
COARSE = 8


epsilon = 1e-06


def shifted(value, axis, steps):
    count = lax.axis_size(axis)
    first, last = (max(0, -steps), min(count, count - steps))
    return lax.ppermute(value, axis, [(source, source + steps) for source in range(first, last)])


def dft_tables(length):
    bin_index = jnp.arange(length, dtype=jnp.int32)
    phase_step = bin_index[:, None] * bin_index[None, :] % length
    angles = phase_step.astype(jnp.float32) * (2.0 * jnp.pi / length)
    return (jnp.cos(angles).astype(jnp.bfloat16), jnp.sin(angles).astype(jnp.bfloat16))


def power_terms(formed):
    values = formed.astype(jnp.float32)
    return jnp.sum(values * values, axis=(1, 3, 4, 6))


def normalise(formed, power_sum, denominator):
    inverse_rms = lax.rsqrt(power_sum / denominator + epsilon)
    return (formed.astype(jnp.float32) * inverse_rms[:, None, :, None, None, :, None]).astype(
        jnp.bfloat16
    )


def correlate(left_beams, right_beams, frames_dev):

    def product(first_part, second_part):
        return jnp.einsum(
            "sbcfpk,tbcfqk->cstbpqk", first_part, second_part, preferred_element_type=jnp.float32
        )

    left_re = left_beams[:, 0]
    left_im = left_beams[:, 1]
    right_re = right_beams[:, 0]
    right_im = right_beams[:, 1]
    vis_re = product(left_re, right_re) + product(left_im, right_im)
    vis_im = product(left_im, right_re) - product(left_re, right_im)
    return jnp.stack([vis_re, vis_im]) / frames_dev


def mixing_of(row_hot, weight_table):
    weights = jnp.einsum("dt,otcb->ocdb", row_hot, weight_table, preferred_element_type=jnp.float32)
    weight_re = weights[0]
    weight_im = weights[1]
    return jnp.stack([jnp.stack([weight_re, -weight_im]), jnp.stack([weight_im, weight_re])])


def per_device(voltages, fir_taps, station_map, beam_index, weight_table):
    components, coarse_dev, dishes_dev, frames_dev, polars, fine_bins = voltages.shape
    history = fir_taps.shape[0] - 1
    table_rows = weight_table.shape[1]
    cosine, sine_table = dft_tables(fine_bins)
    earlier = shifted(voltages[:, :, :, frames_dev - history :], "tm", 1)
    extended = jnp.concatenate([earlier, voltages], axis=3)
    filtered = jnp.zeros(voltages.shape, jnp.float32)
    for tap_index in range(history + 1):
        offset = history - tap_index
        filtered = filtered + fir_taps[tap_index] * extended[
            :, :, :, offset : offset + frames_dev
        ].astype(jnp.float32)
    filtered = filtered.astype(jnp.bfloat16)
    real_part = filtered[0].reshape(-1, fine_bins)
    imag_part = filtered[1].reshape(-1, fine_bins)
    spec_re = jnp.dot(real_part, cosine, preferred_element_type=jnp.float32) + jnp.dot(
        imag_part, sine_table, preferred_element_type=jnp.float32
    )
    spec_im = jnp.dot(imag_part, cosine, preferred_element_type=jnp.float32) - jnp.dot(
        real_part, sine_table, preferred_element_type=jnp.float32
    )
    spectra = jnp.stack([spec_re, spec_im]).reshape(voltages.shape).astype(jnp.bfloat16)
    denominator = COARSE * frames_dev * fine_bins
    own_count = STATIONS // lax.axis_size("stn")
    station_hot = (station_map[:, None] == jnp.arange(STATIONS, dtype=jnp.int32)[None, :]).astype(
        jnp.float32
    )
    table_hot = (beam_index[:, None] == jnp.arange(table_rows, dtype=jnp.int32)[None, :]).astype(
        jnp.bfloat16
    )
    mixing = mixing_of(table_hot, weight_table)
    steering = (station_hot[None, None, None, :, :, None] * mixing[:, :, :, :, None, :]).astype(
        jnp.bfloat16
    )
    full_sums = jnp.einsum(
        "oicdsb,icdfpk->sobcfpk", steering, spectra, preferred_element_type=jnp.float32
    )
    formed = lax.psum(full_sums.astype(jnp.bfloat16), "stn")
    power_sum = lax.psum(power_terms(formed), "chan")
    normed = normalise(formed, power_sum, denominator)
    own_rows = lax.dynamic_slice_in_dim(normed, lax.axis_index("stn") * own_count, own_count, 0)
    visibility = correlate(own_rows, normed, frames_dev)
    return visibility[None]


def solution(mesh):
    in_specs = (
        P(None, "chan", "stn", "tm", None, None),
        P(),
        P("stn"),
        P("stn"),
        P(None, None, "chan", None),
    )
    out_specs = P("tm", None, "chan", "stn", None, None, None, None, None)
    return jax.shard_map(
        per_device, mesh=mesh, in_specs=in_specs, out_specs=out_specs, check_vma=False
    )
```

profile of v0, /device:TPU:0, one launch (start us, length us, event | category | flops | bytes accessed | tf_op | source)
XLA Modules:
  0.0 1312.8 jit_solution(9741827098668168143)
XLA Ops:
  6.5 6.9 slice.122
  21.6 6.4 collective-permute-done
  28.0 6.8 constant_dynamic-update-slice_fusion.1
  34.8 8.4 constant_dynamic-update-slice_fusion
  43.3 108.3 %add_convert_fusion = bf16[2,2,128,16,2,256]{5,4,3,2,1,0:T(2,128)(2,1)} fusion(bf16[2,2,128,16,2,256]{5,4,3,2,1,0:T(2,128)(2,1)S(1)} %bitcast.86, bf16[2,2,128,31,2,256]{5,4,3,2,1,0:T(2,128)(2,1)S(1)} %constant_dynamic-update-slice_fusion, f32[256]{0:T(256)S(1)} %bitcast.102, f32[256]{0:T(256)S(1)} %bitcast.103, f32[256]{0:T(256)S(1)} %bitcast.89, ...), kind=kLoop, calls=%fused_computation.8 | loop fusion | flops 201326592 | bytes 142622720 | tf_op jit(solution)/shard_map/convert_element_type | solution.py:74
  151.6 10.2 fusion.39
  161.8 7.2 reshape_squeeze.6
  168.9 7.2 reshape_squeeze.7
  180.6 5.6 fusion.18
  190.4 7.3 stack.35
  197.8 7.7 copy.19
  205.5 6.4 fusion.3
  211.9 7.2 stack.34
  219.1 5.6 copy.18
  224.7 10.1 fusion.2
  234.9 564.4 %all-reduce.2.cloned.1.call-done = bf16[32,2,8,2,16,2,256]{6,0,2,1,5,4,3:T(8,128)(2,1)} async-done(((bf16[32,2,8,2,16,2,256]{6,0,2,1,5,4,3:T(8,128)(2,1)}), bf16[32,2,8,2,16,2,256]{6,0,2,1,5,4,3:T(8,128)(2,1)}) %all-reduce.2.cloned.1.call-update) | async-done | bytes 16777232 | tf_op jit(solution)/shard_map/psum | solution.py:99
  799.3 7.4 fusion
  806.7 10.0 psum.15
  816.7 12.7 fusion.1
  829.4 6.4 slice_bitcast_fusion
  837.8 22.6 %copy.36 = bf16[8,8,2,16,2,256,1]{3,0,4,6,5,1,2:T(8,128)(2,1)} copy(bf16[8,8,2,16,2,256,1]{5,0,1,4,3,2,6:T(8,128)(2,1)} %get-tuple-element.5) | data formatting | bytes 4194304 | tf_op jit(solution)/shard_map/squeeze | solution.py:45
  860.4 16.6 %copy.38 = bf16[8,8,2,16,2,256,1]{3,0,4,6,5,1,2:T(8,128)(2,1)} copy(bf16[8,8,2,16,2,256,1]{5,0,1,4,3,2,6:T(8,128)(2,1)S(1)} %get-tuple-element.6) | data formatting | bytes 4194304 | tf_op jit(solution)/shard_map/squeeze | solution.py:46
  877.0 44.4 %copy.37 = bf16[32,8,2,16,2,256,1]{0,3,6,4,5,1,2:T(8,128)(2,1)} copy(bf16[32,8,2,16,2,256,1]{5,0,1,4,3,2,6:T(8,128)(2,1)} %get-tuple-element.7) | data formatting | bytes 16777216 | tf_op jit(solution)/shard_map/squeeze | solution.py:48
  921.4 44.4 %copy.35 = bf16[32,8,2,16,2,256,1]{0,3,6,4,5,1,2:T(8,128)(2,1)} copy(bf16[32,8,2,16,2,256,1]{5,0,1,4,3,2,6:T(8,128)(2,1)} %get-tuple-element.8) | data formatting | bytes 16777216 | tf_op jit(solution)/shard_map/squeeze | solution.py:47
  965.8 39.2 %fusion.42 = f32[2,8,256,32,2,8,2]{3,5,6,4,2,1,0:T(8,128)} fusion(bf16[32,8,2,16,2,256,1]{0,3,6,4,5,1,2:T(8,128)(2,1)} %copy.35, bf16[8,8,2,16,2,256,1]{3,0,4,6,5,1,2:T(8,128)(2,1)} %copy.38), kind=kOutput, calls=%fused_computation.70 | convolution fusion | flops 134217728 | bytes 27262976 | tf_op jit(solution)/shard_map/sbcfpk,tbcfqk->cstbpqk/dot_general | solution.py:41
  1005.0 39.2 %fusion.41 = f32[2,8,256,32,2,8,2]{3,5,6,4,2,1,0:T(8,128)} fusion(bf16[32,8,2,16,2,256,1]{0,3,6,4,5,1,2:T(8,128)(2,1)} %copy.35, bf16[8,8,2,16,2,256,1]{3,0,4,6,5,1,2:T(8,128)(2,1)} %copy.36), kind=kOutput, calls=%fused_computation.69 | convolution fusion | flops 134217728 | bytes 27262976 | tf_op jit(solution)/shard_map/sbcfpk,tbcfqk->cstbpqk/dot_general | solution.py:41
  1044.2 60.2 %subtract_bitcast_fusion = f32[1,1,2,8,32,8,2,2,256]{4,3,6,7,8,5,2,1,0:T(8,128)} fusion(f32[2,8,256,32,2,8,2]{3,5,6,4,2,1,0:T(8,128)} %fusion.42, bf16[32,8,2,16,2,256,1]{0,3,6,4,5,1,2:T(8,128)(2,1)} %copy.37, bf16[8,8,2,16,2,256,1]{3,0,4,6,5,1,2:T(8,128)(2,1)} %copy.36), kind=kOutput, calls=%fused_computation | convolution fusion | flops 138412032 | bytes 44040192 | tf_op jit(solution)/shard_map/sbcfpk,tbcfqk->cstbpqk/dot_general | solution.py:41
  1104.4 34.7 %copy.30 = f32[1,1,2,8,32,8,2,2,256]{8,5,7,6,4,3,2,1,0:T(8,128)} copy(f32[1,1,2,8,32,8,2,2,256]{4,3,6,7,8,5,2,1,0:T(8,128)} %subtract_bitcast_fusion) | data formatting | bytes 33554432 | tf_op jit(solution)/shard_map/stack | solution.py:51
  1139.1 60.5 %add_bitcast_fusion = f32[1,1,2,8,32,8,2,2,256]{4,3,6,7,8,5,2,1,0:T(8,128)} fusion(f32[2,8,256,32,2,8,2]{3,5,6,4,2,1,0:T(8,128)} %fusion.41, bf16[32,8,2,16,2,256,1]{0,3,6,4,5,1,2:T(8,128)(2,1)} %copy.37, bf16[8,8,2,16,2,256,1]{3,0,4,6,5,1,2:T(8,128)(2,1)} %copy.38), kind=kOutput, calls=%fused_computation.1 | convolution fusion | flops 138412032 | bytes 44040192 | tf_op jit(solution)/shard_map/sbcfpk,tbcfqk->cstbpqk/dot_general | solution.py:41
  1199.5 34.8 %copy.29 = f32[1,1,2,8,32,8,2,2,256]{8,5,7,6,4,3,2,1,0:T(8,128)} copy(f32[1,1,2,8,32,8,2,2,256]{4,3,6,7,8,5,2,1,0:T(8,128)} %add_bitcast_fusion) | data formatting | bytes 33554432 | tf_op jit(solution)/shard_map/stack | solution.py:51
  1234.3 24.9 %maximum_multiply_fusion = f32[1,2,2,8,32,8,2,2,256]{8,5,7,6,4,3,2,1,0:T(8,128)} fusion(f32[1,1,2,8,32,8,2,2,256]{8,5,7,6,4,3,2,1,0:T(8,128)} %copy.30, f32[1,1,2,8,32,8,2,2,256]{8,5,7,6,4,3,2,1,0:T(8,128)} %copy.29), kind=kLoop, calls=%fused_computation.6 | loop fusion | flops 16777216 | bytes 67108864 | tf_op jit(solution)/shard_map/div | solution.py:51
  1259.2 46.3 %copy.31 = f32[1,2,2,8,32,8,2,2,256]{8,7,6,5,4,3,2,1,0:T(2,128)} copy(f32[1,2,2,8,32,8,2,2,256]{8,5,7,6,4,3,2,1,0:T(8,128)} %maximum_multiply_fusion) | data formatting | bytes 67108864 | tf_op jit(solution)/shard_map/div | solution.py:51
  (27 shorter events, 18.8 us)
Async XLA Ops:
  6.5 12.4 copy-start
  6.5 792.8 %all-reduce.2.cloned.1.call-start = ((), (), s32[]{:S(2)}) async-start(), calls=%async_computation | async-start | bytes 33554432 | tf_op jit(solution)/shard_map/psum | solution.py:99
  6.5 28.2 %slice-start = ((s8[8388608]{0:T(1024)(128)(4,1)}), s8[4194304]{0:T(1024)(128)(4,1)S(1)}, s32[]{:S(2)}) async-start(s8[8388608]{0:T(1024)(128)(4,1)} %bitcast.85), calls=%async_computation.1 | async-start | bytes 8388608
  13.5 14.6 %collective-permute-start = (bf16[2,2,128,15,2,256]{5,4,3,2,1,0:T(2,128)(2,1)S(1)}, bf16[2,2,128,15,2,256]{5,4,3,2,1,0:T(2,128)(2,1)}, u32[]{:S(2)}, u32[]{:S(2)}) collective-permute-start(bf16[2,2,128,15,2,256]{5,4,3,2,1,0:T(2,128)(2,1)S(1)} %slice.122), channel_id=1, source_target_pairs={{0,16},{1,17},{2,18},{3,19},{4,20},{5,21},{6,22},{7,23},{8,24},{9,... | collective-permute-start | bytes 23592968 | tf_op jit(solution)/shard_map/ppermute | solution.py:16
  19.7 15.1 %slice-start.1 = ((s8[8388608]{0:T(1024)(128)(4,1)}), s8[4194304]{0:T(1024)(128)(4,1)S(1)}, s32[]{:S(2)}) async-start(s8[8388608]{0:T(1024)(128)(4,1)} %bitcast.85), calls=%async_computation.2 | async-start | bytes 8388608
  176.1 4.5 copy-start.3
  197.8 7.7 copy-start.2
  1259.2 46.3 %copy-start.1 = (bf16[2,16,2,8]{1,3,2,0:T(8,128)(2,1)S(1)}, bf16[2,16,2,8]{1,3,2,0:T(8,128)(2,1)}, u32[]{:S(2)}) copy-start(bf16[2,16,2,8]{1,3,2,0:T(8,128)(2,1)} %param.9) | copy-start | bytes 3076
Sparse Core Ops, SparseCore 0:
  235.0 564.2 all-reduce.1
where the time goes:
time: 1320 us; the launch traced here: 1310 us
  waiting for transfers between devices  571 us (43%)
  local copies, waits for them, and re-layouts  328 us (25%)
  matrix products  231 us (18%)
  other arithmetic  154 us (12%)
  between operations  14 us (1%)
    psum x1, waiting for transfers between devices, per_device(): formed = lax.psum(full_sums.astype(jnp.bfloat16), 'stn')  564 us
    dot_general x4, matrix products, product(): jnp.einsum('sbcfpk,tbcfqk->cstbpqk', first_part, second_part, preferred_e...  199 us
    convert_element_type x1, other arithmetic, per_device(): filtered = filtered.astype(jnp.bfloat16)  108 us
    another operation x2, local copies, waits for them, and re-layouts, correlate(): return jnp.stack([vis_re, vis_im]) / frames_dev  69.5 us
    squeeze x2, local copies, waits for them, and re-layouts, correlate(): right_im = right_beams[:, 1]  50.9 us
    div x1, local copies, waits for them, and re-layouts, correlate(): return jnp.stack([vis_re, vis_im]) / frames_dev  46.3 us
    squeeze x1, local copies, waits for them, and re-layouts, correlate(): right_re = right_beams[:, 0]  44.4 us
    another operation x4, local copies, waits for them, and re-layouts, per_device(): jnp.stack([spec_re, spec_im]).reshape(voltages.shape).astype(jnp.bfloat16)  27.9 us
  transfers between devices with their start and end apart: 2, of which 2 were waited for; matrix products, arithmetic and copies ran while one was open for 0% of the time, Pallas kernels for 0%

commit v1 on v0

v1 whole, which is shorter than its diff:
```python
import functools

import jax
import jax.numpy as jnp
from jax import lax
from jax.experimental import pallas as pl
from jax.experimental.pallas import tpu as pltpu
from jax.sharding import PartitionSpec as P

STATIONS = 32
COARSE = 8
LANES = 128
VMEM_LIMIT = 60 * 1024 * 1024

epsilon = 1e-06


def shifted(value, axis, steps):
    count = lax.axis_size(axis)
    first, last = (max(0, -steps), min(count, count - steps))
    return lax.ppermute(value, axis, [(source, source + steps) for source in range(first, last)])


def dft_table(length):
    bin_index = jnp.arange(length, dtype=jnp.int32)
    phase_step = bin_index[:, None] * bin_index[None, :] % length
    angles = phase_step.astype(jnp.float32) * (2.0 * jnp.pi / length)
    cosine = jnp.cos(angles).astype(jnp.bfloat16)
    sine = jnp.sin(angles).astype(jnp.bfloat16)
    top = jnp.concatenate([cosine, -sine], axis=1)
    return jnp.concatenate([top, jnp.concatenate([sine, cosine], axis=1)], axis=0)


def spectra_kernel(n_dest, x_ref, taps_ref, dft_ref, perm_ref, out_ref, fil_ref):
    taps = taps_ref.shape[0]
    frames = out_ref.shape[2]
    dishes, fine = x_ref.shape[3], x_ref.shape[4]
    share = dishes // n_dest
    rows = min(32, dishes)
    group = 2

    def step(i, carry):
        for j in range(group):
            frame = i * group + j
            for o in range(2):
                for low in range(0, dishes, rows):
                    total = jnp.zeros((rows, fine), jnp.float32)
                    for tap in range(taps):
                        sample = x_ref[0, frame + (taps - 1 - tap), o, low : low + rows, :]
                        total = total + taps_ref[tap : tap + 1, :] * sample.astype(jnp.float32)
                    fil_ref[
                        j * dishes + low : j * dishes + low + rows, o * fine : (o + 1) * fine
                    ] = total.astype(jnp.bfloat16)
        spec = jnp.dot(fil_ref[...], dft_ref[...], preferred_element_type=jnp.float32)
        spec = spec.astype(jnp.bfloat16)
        for j in range(group):
            moved = jnp.dot(
                perm_ref[...],
                spec[j * dishes : (j + 1) * dishes],
                preferred_element_type=jnp.float32,
            )
            for dest in range(n_dest):
                for o in range(2):
                    out_ref[dest, 0, i * group + j, o] = moved[
                        dest * share : (dest + 1) * share, o * fine : (o + 1) * fine
                    ].astype(jnp.bfloat16)
        return carry

    lax.fori_loop(0, frames // group, step, 0)


def spectra_of(extended, fir_taps, table, perm, n_dest, frames):
    polars, total_frames, _, dishes, fine = extended.shape
    share = dishes // n_dest
    flops = 2 * polars * frames * dishes * (2 * fine) * (2 * fine + dishes)
    return pl.pallas_call(
        functools.partial(spectra_kernel, n_dest),
        grid=(polars,),
        in_specs=[
            pl.BlockSpec((1, total_frames, 2, dishes, fine), lambda p: (p, 0, 0, 0, 0)),
            pl.BlockSpec(fir_taps.shape, lambda p: (0, 0)),
            pl.BlockSpec(table.shape, lambda p: (0, 0)),
            pl.BlockSpec(perm.shape, lambda p: (0, 0)),
        ],
        out_specs=pl.BlockSpec(
            (n_dest, 1, frames, 2, share, fine), lambda p: (0, p, 0, 0, 0, 0)
        ),
        out_shape=jax.ShapeDtypeStruct((n_dest, polars, frames, 2, share, fine), jnp.bfloat16),
        scratch_shapes=[pltpu.VMEM((2 * dishes, 2 * fine), jnp.bfloat16)],
        compiler_params=pltpu.CompilerParams(vmem_limit_bytes=VMEM_LIMIT),
        cost_estimate=pl.CostEstimate(
            flops=flops * 4, bytes_accessed=extended.size * 4, transcendentals=0
        ),
        name="spectra",
    )(extended, fir_taps, table, perm)


def beams_kernel(x_ref, steer_ref, out_ref, power_ref):
    frames, fine = out_ref.shape[1], out_ref.shape[3]
    power_ref[...] = jnp.zeros_like(power_ref)

    def step(frame, carry):
        terms = x_ref[:, 0, frame]
        if terms.shape[2] % 16:
            terms = terms.astype(jnp.float32).reshape(-1, fine).astype(jnp.bfloat16)
        else:
            terms = terms.reshape(-1, fine)
        formed = jnp.dot(steer_ref[...], terms, preferred_element_type=jnp.float32)
        formed = formed.astype(jnp.bfloat16)
        out_ref[0, frame] = formed
        wide = formed.astype(jnp.float32)
        power_ref[0] += wide * wide
        return carry

    lax.fori_loop(0, frames, step, 0)


def beams_of(spectra, steering):
    groups, polars, frames, _, share, fine = spectra.shape
    rows = steering.shape[0]
    return pl.pallas_call(
        beams_kernel,
        grid=(polars,),
        in_specs=[
            pl.BlockSpec((groups, 1, frames, 2, share, fine), lambda p: (0, p, 0, 0, 0, 0)),
            pl.BlockSpec(steering.shape, lambda p: (0, 0)),
        ],
        out_specs=[
            pl.BlockSpec((1, frames, rows, fine), lambda p: (p, 0, 0, 0)),
            pl.BlockSpec((1, rows, fine), lambda p: (p, 0, 0)),
        ],
        out_shape=[
            jax.ShapeDtypeStruct((polars, frames, rows, fine), jnp.bfloat16),
            jax.ShapeDtypeStruct((polars, rows, fine), jnp.float32),
        ],
        compiler_params=pltpu.CompilerParams(vmem_limit_bytes=VMEM_LIMIT),
        cost_estimate=pl.CostEstimate(
            flops=2 * rows * steering.shape[1] * polars * frames * fine,
            bytes_accessed=spectra.size * 4,
            transcendentals=0,
        ),
        name="beams",
    )(spectra, steering)


def correlate_kernel(beams, left_ref, right_ref, lscale_ref, rscale_ref, *rest):
    out_ref, left, right = rest[-3:]
    polars, frames, rows, fine = left_ref.shape
    own = rows // (2 * beams)
    halves = fine // LANES
    first = pl.program_id(0) == 0

    def widen(source, target):
        def step(i, carry):
            for p in range(polars):
                target[p, i] = source(p, i).astype(jnp.float32)
            return carry

        lax.fori_loop(0, frames, step, 0)

    @pl.when(first)
    def _():
        widen(lambda p, i: left_ref[p, i], left)

    widen(lambda p, i: right_ref[0, p, i], right)

    def pair(index, carry):
        s = index // own
        t = index % own
        srow = pl.multiple_of(s * (2 * beams), 2 * beams)
        trow = pl.multiple_of(t * (2 * beams), 2 * beams)
        for half in range(halves):
            lanes = pl.ds(half * LANES, LANES)
            re = {}
            im = {}
            for f in range(frames):
                lre = [left[p, f, pl.ds(srow, beams), lanes] for p in range(polars)]
                lim = [left[p, f, pl.ds(srow + beams, beams), lanes] for p in range(polars)]
                rre = [right[q, f, pl.ds(trow, beams), lanes] for q in range(polars)]
                rim = [right[q, f, pl.ds(trow + beams, beams), lanes] for q in range(polars)]
                for p in range(polars):
                    for q in range(polars):
                        a = lre[p] * rre[q] + lim[p] * rim[q]
                        b = lim[p] * rre[q] - lre[p] * rim[q]
                        re[p, q] = a if f == 0 else re[p, q] + a
                        im[p, q] = b if f == 0 else im[p, q] + b
            for p in range(polars):
                for q in range(polars):
                    scale = lscale_ref[p, s] * rscale_ref[0, q, t]
                    row = (p * halves + half) * polars + q
                    where = pl.ds(row, beams, stride=polars * polars * halves)
                    out_ref[0, 0, s, t, where, :] = re[p, q] * scale
                    out_ref[1, 0, s, t, where, :] = im[p, q] * scale
        return carry

    lax.fori_loop(0, own * own, pair, 0)


def correlate(index, coarse_dev, beams, left, right, lscale, rscale, previous):
    groups, polars, frames, rows, fine = right.shape
    own = rows // (2 * beams)
    out_rows = beams * polars * polars * (fine // LANES)
    shape = (2, coarse_dev, own, groups * own, out_rows, LANES)
    in_specs = [
        pl.BlockSpec((polars, frames, rows, fine), lambda g: (0, 0, 0, 0)),
        pl.BlockSpec((1, polars, frames, rows, fine), lambda g: (g, 0, 0, 0, 0)),
        pl.BlockSpec(lscale.shape, lambda g: (0, 0, 0, 0)),
        pl.BlockSpec((1,) + rscale.shape[1:], lambda g: (g, 0, 0, 0, 0)),
    ]
    operands = [left, right, lscale, rscale]
    aliases = {}
    if previous is not None:
        in_specs.append(pl.BlockSpec(memory_space=pl.ANY))
        operands.append(previous)
        aliases = {4: 0}
    size = 2 * own * groups * own * out_rows * LANES
    return pl.pallas_call(
        functools.partial(correlate_kernel, beams),
        grid=(groups,),
        in_specs=in_specs,
        out_specs=pl.BlockSpec(
            (2, 1, own, own, out_rows, LANES), lambda g: (0, index, 0, g, 0, 0)
        ),
        out_shape=jax.ShapeDtypeStruct(shape, jnp.float32),
        scratch_shapes=[
            pltpu.VMEM((polars, frames, rows, fine), jnp.float32),
            pltpu.VMEM((polars, frames, rows, fine), jnp.float32),
        ],
        input_output_aliases=aliases,
        compiler_params=pltpu.CompilerParams(vmem_limit_bytes=VMEM_LIMIT),
        cost_estimate=pl.CostEstimate(
            flops=size * 4 * frames * 100, bytes_accessed=size * 4, transcendentals=0
        ),
        name="correlate",
    )(*operands)


def routes(station_map, beam_index, own_count):
    block = station_map // own_count
    groups, dishes = station_map.shape
    order = jnp.arange(dishes, dtype=jnp.int32)
    same = block[:, :, None] == block[:, None, :]
    before = order[None, None, :] < order[None, :, None]
    rank = jnp.sum((same & before).astype(jnp.int32), axis=2)
    place = block * (dishes // groups) + rank
    hot = place[:, None, :] == order[None, :, None]
    station = jnp.sum(jnp.where(hot, station_map[:, None, :], 0), axis=2)
    row = jnp.sum(jnp.where(hot, beam_index[:, None, :], 0), axis=2)
    return hot, station, row


def per_device(voltages, fir_taps, station_map, beam_index, weight_table):
    components, coarse_dev, dishes_dev, frames_dev, polars, fine = voltages.shape
    history = fir_taps.shape[0] - 1
    table_rows, beams = weight_table.shape[1], weight_table.shape[3]
    groups = lax.axis_size("stn")
    own_count = STATIONS // groups
    share = dishes_dev // groups
    me = lax.axis_index("stn")
    earlier = shifted(voltages[:, :, :, frames_dev - history :], "tm", 1)
    table = dft_table(fine)
    both = lax.all_gather(jnp.stack([station_map, beam_index]), "stn")
    hot, station, row = routes(both[:, 0], both[:, 1], own_count)
    perm = lax.dynamic_index_in_dim(hot, me, 0, keepdims=False).astype(jnp.bfloat16)
    station = lax.dynamic_slice_in_dim(station, me * share, share, 1)
    row = lax.dynamic_slice_in_dim(row, me * share, share, 1)
    station_hot = (
        station[:, :, None] - me * own_count == jnp.arange(own_count, dtype=jnp.int32)
    ).astype(jnp.float32)
    table_hot = (row[:, :, None] == jnp.arange(table_rows, dtype=jnp.int32)).astype(jnp.bfloat16)
    weights = jnp.einsum(
        "gdt,otcb->ocgdb", table_hot, weight_table, preferred_element_type=jnp.float32
    )
    mixing = jnp.stack(
        [jnp.stack([weights[0], -weights[1]]), jnp.stack([weights[1], weights[0]])]
    )
    steering = jnp.einsum("gds,oicgdb->csobgid", station_hot, mixing).astype(jnp.bfloat16)
    steering = steering.reshape(coarse_dev, own_count * 2 * beams, groups * 2 * share)

    formed = []
    gathered = []
    power = 0.0
    spectra = []
    for c in range(coarse_dev):
        extended = jnp.concatenate([earlier[:, c], voltages[:, c]], axis=2)
        extended = jnp.transpose(extended, (3, 2, 0, 1, 4))
        terms = spectra_of(extended, fir_taps, table, perm, groups, frames_dev)
        spectra.append(lax.all_to_all(terms, "stn", 0, 0))
    for c in range(coarse_dev):
        values, squares = beams_of(spectra[c], steering[c])
        formed.append(values)
        gathered.append(lax.all_gather(values, "stn"))
        power = power + jnp.sum(squares.reshape(polars, own_count, 2, beams, fine), axis=(2, 4))
    power = lax.psum(power, "chan")
    inverse_rms = lax.rsqrt(power / (COARSE * frames_dev * fine) + epsilon)
    every = lax.all_gather(inverse_rms, "stn")
    lscale = jnp.broadcast_to(
        inverse_rms[..., None] / frames_dev, inverse_rms.shape + (LANES,)
    )
    rscale = jnp.broadcast_to(every[..., None], every.shape + (LANES,))
    result = None
    for c in range(coarse_dev):
        result = correlate(
            c, coarse_dev, beams, formed[c], gathered[c], lscale, rscale, result
        )
    halves = fine // LANES
    result = result.reshape(
        2, coarse_dev, own_count, STATIONS, beams, polars, halves, polars, LANES
    )
    result = jnp.swapaxes(result, 6, 7)
    return result.reshape(
        1, 2, coarse_dev, own_count, STATIONS, beams, polars, polars, fine
    )


def solution(mesh):
    in_specs = (
        P(None, "chan", "stn", "tm", None, None),
        P(),
        P("stn"),
        P("stn"),
        P(None, None, "chan", None),
    )
    out_specs = P("tm", None, "chan", "stn", None, None, None, None, None)
    return jax.shard_map(
        per_device, mesh=mesh, in_specs=in_specs, out_specs=out_specs, check_vma=False
    )
```

time: 1320 us -> 656 us (0.50)
  local copies, waits for them, and re-layouts: 328 us -> 41.4 us
  waiting for transfers between devices: 571 us -> 334 us
  matrix products: 231 us -> 0.13 us
  Pallas kernels: 0 us -> 190 us
  other arithmetic: 154 us -> 21.2 us
  blocking collectives: 10 us -> 38.8 us
    psum x1 -> x0, waiting for transfers between devices: 564 us -> none  [per_device(): formed = lax.psum(full_sums.astype(jnp.bfloat16), 'stn')]
    all_to_all x0 -> x2, waiting for transfers between devices: none -> 276 us  [per_device(): spectra.append(lax.all_to_all(terms, 'stn', 0, 0))]
    dot_general x9 -> x1, matrix products: 230 us -> 0.13 us  [per_device(): jnp.einsum('gdt,otcb->ocgdb', table_hot, weight_table, preferred_element_...]
    pallas_call x0 -> x6, Pallas kernels: none -> 190 us  [the longest x2 129 us: correlate(): pl.pallas_call(functools.partial(correlate_kernel, beams), grid=(groups,)...]
    convert_element_type x3, other arithmetic: 122 us -> 2.21 us  [the longest x1 1.1 us: dft_table(): sine = jnp.sin(angles).astype(jnp.bfloat16)]
    squeeze x6 -> x4, local copies, waits for them, and re-layouts: 136 us -> 18.7 us  [the longest x2 17 us: per_device(): extended = jnp.concatenate([earlier[:, c], voltages[:, c]], axis=2)]
    another operation x9 -> x1, local copies, waits for them, and re-layouts: 112 us -> 0.07 us  [per_device(): jnp.stack([jnp.stack([weights[0], -weights[1]]), jnp.stack([weights[1], w...]
    all_gather x0 -> x2, waiting for transfers between devices: none -> 58.1 us  [per_device(): gathered.append(lax.all_gather(values, 'stn'))]
  transfers between devices with their start and end apart: 2 -> 5, of which waited for: 2 -> 3; matrix products, arithmetic and copies ran while one was open for 0% -> 6% of each run, Pallas kernels for 0% -> 15%
where the time goes in v1:
time: 656 us; the launch traced here: 655 us
  waiting for transfers between devices  334 us (51%)
  Pallas kernels  190 us (29%)
  local copies, waits for them, and re-layouts  41.4 us (6%)
  blocking collectives  38.8 us (6%)
  other arithmetic  21.2 us (3%)
  starting transfers between devices  15.5 us (2%)
  between operations  13.6 us (2%)
    all_to_all x2, waiting for transfers between devices, per_device(): spectra.append(lax.all_to_all(terms, 'stn', 0, 0))  276 us
    pallas_call x2, Pallas kernels, correlate(): pl.pallas_call(functools.partial(correlate_kernel, beams), grid=(groups,)...  129 us
    all_gather x2, waiting for transfers between devices, per_device(): gathered.append(lax.all_gather(values, 'stn'))  58.1 us
    pallas_call x2, Pallas kernels, spectra_of(): pl.pallas_call(functools.partial(spectra_kernel, n_dest), grid=(polars,),...  44.8 us
    squeeze x2, local copies, waits for them, and re-layouts, per_device(): extended = jnp.concatenate([earlier[:, c], voltages[:, c]], axis=2)  17 us
    all_gather x1, blocking collectives, per_device(): every = lax.all_gather(inverse_rms, 'stn')  16.8 us
    pallas_call x2, Pallas kernels, beams_of(): pl.pallas_call(beams_kernel, grid=(polars,), in_specs=[pl.BlockSpec((grou...  16.6 us
    transpose x2, other arithmetic, per_device(): extended = jnp.transpose(extended, (3, 2, 0, 1, 4))  15.1 us
  transfers between devices with their start and end apart: 5, of which 3 were waited for; matrix products, arithmetic and copies ran while one was open for 6% of the time, Pallas kernels for 15%

profile of v1, /device:TPU:0, one launch (start us, length us, event | category | flops | bytes accessed | tf_op | source)
XLA Modules:
  0.0 655.4 jit_solution(9802897720523020236)
XLA Ops:
  6.5 6.8 %slice.37 = bf16[2,2,128,15,2,256]{5,4,3,2,1,0:T(2,128)(2,1)S(1)} slice(bf16[2,2,128,16,2,256]{5,4,3,2,1,0:T(2,128)(2,1)} %param.5), slice={[0:2], [0:2], [0:128], [1:16], [0:2], [0:256]} | slice | bytes 15728640 | tf_op jit(solution)/shard_map/slice | solution.py:260
  13.3 4.9 copy.34
  18.3 5.5 collective-permute-start
  23.7 12.0 %all-gather.4 = s32[4,2,128]{2,1,0:T(2,128)S(1)} all-gather(s32[1,2,128]{2,1,0:T(2,128)S(1)} %add_bitcast_fusion), channel_id=2, replica_groups=mesh['tm'=2,'stn'=4,'chan'=4] {'stn'}, dimensions={0}, use_global_device_ids=true | all-gather | bytes 5120 | tf_op jit(solution)/shard_map/all_gather | solution.py:262
  36.1 0.6 fusion.8.perm_ref
  36.7 1.0 fusion.7
  37.7 1.1 sine_convert_fusion
  38.8 0.9 maximum_maximum_fusion.dft_ref
  39.7 8.6 %fusion.20 = (bf16[2,1,128,16,2,256]{5,4,3,2,1,0:T(2,128)(2,1)S(1)}, bf16[2,1,128,16,2,256]{5,4,3,2,1,0:T(2,128)(2,1)S(1)}) fusion(bf16[2,2,128,16,2,256]{5,4,3,2,1,0:T(2,128)(2,1)} %param.5), kind=kLoop, calls=%fused_computation.61 | loop fusion | bytes 16777216 | tf_op jit(solution)/shard_map/slice | solution.py:285
  48.3 11.4 %copy_bitcast_fusion = (bf16[2,128,16,2,256]{4,1,0,2,3:T(8,128)(2,1)}, bf16[2,128,16,2,256]{4,1,0,2,3:T(8,128)(2,1)}) fusion(bf16[2,1,128,16,2,256]{5,4,3,2,1,0:T(2,128)(2,1)S(1)} %get-tuple-element.16, bf16[2,1,128,16,2,256]{5,4,3,2,1,0:T(2,128)(2,1)S(1)} %get-tuple-element.15), kind=kLoop, calls=%fused_computation.2 | loop fusion | bytes 16777216 | tf_op jit(solution)/shard_map/squeeze | solution.py:285
  59.8 5.6 slice_bitcast_fusion
  65.4 7.4 %maximum_bitcast_fusion.1.x_ref = bf16[2,31,2,128,256]{4,3,2,1,0:T(8,128)(2,1)} fusion(bf16[2,128,16,2,256]{4,1,0,2,3:T(8,128)(2,1)} %get-tuple-element.31, bf16[2,128,15,2,256]{4,1,0,2,3:T(8,128)(2,1)} %get-tuple-element.17), kind=kLoop, calls=%fused_computation.1 | loop fusion | flops 4063232 | bytes 16252928 | tf_op jit(solution)/shard_map/transpose | solution.py:286
  72.8 22.2 %spectra.3 = bf16[4,2,16,2,32,256]{5,4,3,2,1,0:T(8,128)(2,1)} custom-call(bf16[2,31,2,128,256]{4,3,2,1,0:T(8,128)(2,1)} %maximum_bitcast_fusion.1.x_ref, f32[16,256]{1,0:T(8,128)} %taps_ref.3, bf16[512,512]{1,0:T(8,128)(2,1)} %maximum_maximum_fusion.dft_ref, bf16[128,128]{1,0:T(8,128)(2,1)} %fusion.8.perm_ref), custom_call_target="tpu_custom_call" | custom-call | flops 10737418240 | bytes 16252928 | tf_op jit(solution)/shard_map/spectra/pallas_call | solution.py:76
  94.9 4.8 all-to-all-start.1
  100.7 0.5 fusion
  101.6 0.8 squeeze.30.steer_ref
  102.4 85.3 %all-to-all-done.1.x_ref = bf16[4,2,16,2,32,256]{5,4,3,2,1,0:T(8,128)(2,1)} async-done(((bf16[4,2,16,2,32,256]{5,4,3,2,1,0:T(8,128)(2,1)}), bf16[4,2,16,2,32,256]{5,4,3,2,1,0:T(8,128)(2,1)}, u32[]{:S(2)}, u32[]{:S(2)}) %all-to-all-start.1) | async-done | bytes 4194336 | tf_op jit(solution)/shard_map/all_to_all | solution.py:288
  187.7 8.3 %beams.3 = (bf16[2,16,128,256]{3,2,1,0:T(8,128)(2,1)}, f32[2,128,256]{2,1,0:T(8,128)}) custom-call(bf16[4,2,16,2,32,256]{5,4,3,2,1,0:T(8,128)(2,1)} %all-to-all-done.1.x_ref, bf16[128,256]{1,0:T(8,128)(2,1)} %squeeze.30.steer_ref), custom_call_target="tpu_custom_call" | custom-call | flops 536870912 | bytes 8388608 | tf_op jit(solution)/shard_map/beams/pallas_call | solution.py:121
  196.1 7.7 %maximum_bitcast_fusion.x_ref = bf16[2,31,2,128,256]{4,3,2,1,0:T(8,128)(2,1)} fusion(bf16[2,128,16,2,256]{4,1,0,2,3:T(8,128)(2,1)} %get-tuple-element.30, bf16[2,128,15,2,256]{4,1,0,2,3:T(8,128)(2,1)} %get-tuple-element.18), kind=kLoop, calls=%fused_computation | loop fusion | flops 4063232 | bytes 16252928 | tf_op jit(solution)/shard_map/transpose | solution.py:286
  203.8 22.6 %spectra.2 = bf16[4,2,16,2,32,256]{5,4,3,2,1,0:T(8,128)(2,1)} custom-call(bf16[2,31,2,128,256]{4,3,2,1,0:T(8,128)(2,1)} %maximum_bitcast_fusion.x_ref, f32[16,256]{1,0:T(8,128)} %taps_ref.3, bf16[512,512]{1,0:T(8,128)(2,1)} %maximum_maximum_fusion.dft_ref, bf16[128,128]{1,0:T(8,128)(2,1)} %fusion.8.perm_ref), custom_call_target="tpu_custom_call" | custom-call | flops 10737418240 | bytes 16252928 | tf_op jit(solution)/shard_map/spectra/pallas_call | solution.py:76
  226.4 4.9 all-to-all-start
  231.4 0.8 squeeze.27.steer_ref
  232.2 190.9 %all-to-all-done.x_ref = bf16[4,2,16,2,32,256]{5,4,3,2,1,0:T(8,128)(2,1)} async-done(((bf16[4,2,16,2,32,256]{5,4,3,2,1,0:T(8,128)(2,1)}), bf16[4,2,16,2,32,256]{5,4,3,2,1,0:T(8,128)(2,1)}, u32[]{:S(2)}, u32[]{:S(2)}) %all-to-all-start) | async-done | bytes 4194336 | tf_op jit(solution)/shard_map/all_to_all | solution.py:288
  423.2 8.3 %beams.2 = (bf16[2,16,128,256]{3,2,1,0:T(8,128)(2,1)}, f32[2,128,256]{2,1,0:T(8,128)}) custom-call(bf16[4,2,16,2,32,256]{5,4,3,2,1,0:T(8,128)(2,1)} %all-to-all-done.x_ref, bf16[128,256]{1,0:T(8,128)(2,1)} %squeeze.27.steer_ref), custom_call_target="tpu_custom_call" | custom-call | flops 536870912 | bytes 8388608 | tf_op jit(solution)/shard_map/beams/pallas_call | solution.py:121
  431.5 1.1 reduce_sum.68
  433.0 10.0 %psum.7 = f32[2,8,8]{2,1,0:T(8,128)S(1)} all-reduce(f32[2,8,8]{2,1,0:T(8,128)S(1)} %add.46), channel_id=1, replica_groups=mesh['tm'=2,'stn'=4,'chan'=4] {'chan'}, use_global_device_ids=true, to_apply=%region_7.8 | all-reduce | flops 128 | bytes 1024 | tf_op jit(solution)/shard_map/psum | solution.py:294
  443.0 16.8 %all-gather.2 = f32[8,8,8]{2,1,0:T(8,128)S(1)} all-gather(f32[2,8,8]{2,1,0:T(8,128)S(1)} %get-tuple-element.26), channel_id=4, replica_groups=mesh['tm'=2,'stn'=4,'chan'=4] {'stn'}, dimensions={0}, use_global_device_ids=true | all-gather | bytes 2560 | tf_op jit(solution)/shard_map/all_gather | solution.py:296
  459.8 0.7 broadcast_in_dim.48.lscale_ref
  460.5 0.8 broadcast_in_dim.49.rscale_ref
  461.3 64.6 %correlate.2.rest_0_ = f32[2,2,8,32,64,128]{5,4,3,2,1,0:T(8,128)} custom-call(bf16[2,16,128,256]{3,2,1,0:T(8,128)(2,1)} %get-tuple-element.12.left_ref, bf16[4,2,16,128,256]{4,3,2,1,0:T(8,128)(2,1)} %bitcast.64, f32[2,8,8,128]{3,2,1,0:T(8,128)} %broadcast_in_dim.48.lscale_ref, f32[4,2,8,8,128]{4,3,2,1,0:T(8,128)} %broadcast_in_dim.49.rscale_ref), custom_call_target="tpu_custom_call" | custom-call | flops 26843545600 | bytes 16777216 | tf_op jit(solution)/shard_map/correlate/pallas_call | solution.py:217
  525.9 58.1 %all-gather.8.cloned.1.call-done = bf16[8,16,128,256]{3,2,1,0:T(8,128)(2,1)} async-done(((bf16[2,16,128,256]{3,2,1,0:T(8,128)(2,1)}), bf16[8,16,128,256]{3,2,1,0:T(8,128)(2,1)}) %all-gather.8.cloned.1.call-update) | async-done | bytes 8388624 | tf_op jit(solution)/shard_map/all_gather | solution.py:292
  584.0 64.5 %correlate.3 = f32[2,2,8,32,64,128]{5,4,3,2,1,0:T(8,128)} custom-call(bf16[2,16,128,256]{3,2,1,0:T(8,128)(2,1)} %get-tuple-element.9.left_ref, bf16[4,2,16,128,256]{4,3,2,1,0:T(8,128)(2,1)} %bitcast.65, f32[2,8,8,128]{3,2,1,0:T(8,128)} %broadcast_in_dim.48.lscale_ref, ...), custom_call_target="tpu_custom_call", output_to_operand_aliasing={{}: (4, {})} | custom-call | flops 26843545600 | bytes 16777216 | tf_op jit(solution)/shard_map/correlate/pallas_call | solution.py:217
  (41 shorter events, 2.1 us)
Async XLA Ops:
  6.5 93.8 %copy-start = (bf16[2,16,2,8]{1,3,2,0:T(8,128)(2,1)S(1)}, bf16[2,16,2,8]{1,3,2,0:T(8,128)(2,1)}, u32[]{:S(2)}) copy-start(bf16[2,16,2,8]{1,3,2,0:T(8,128)(2,1)} %param.9) | copy-start | bytes 3076
  13.3 10.4 %copy-start.3 = (s32[128]{0:T(128)S(1)}, s32[128]{0:T(128)}, u32[]{:S(2)}) copy-start(s32[128]{0:T(128)} %param.8) | copy-start | bytes 1540
  13.3 10.4 %copy-start.4 = (s32[128]{0:T(128)S(1)}, s32[128]{0:T(128)}, u32[]{:S(2)}) copy-start(s32[128]{0:T(128)} %param.7) | copy-start | bytes 1540
  18.3 41.5 %collective-permute-start = (bf16[2,2,128,15,2,256]{5,2,0,3,4,1:T(8,128)(2,1)}, bf16[2,2,128,15,2,256]{5,2,0,3,4,1:T(8,128)(2,1)}, u32[]{:S(2)}, u32[]{:S(2)}) collective-permute-start(bf16[2,2,128,15,2,256]{5,2,0,3,4,1:T(8,128)(2,1)} %copy.34), channel_id=1, source_target_pairs={{0,16},{1,17},{2,18},{3,19},{4,20},{5,21},{6,22},{7,23},{8,24},{9,... | collective-permute-start | bytes 23592968 | tf_op jit(solution)/shard_map/ppermute | solution.py:21
  94.9 92.8 %all-to-all-start.1 = ((bf16[4,2,16,2,32,256]{5,4,3,2,1,0:T(8,128)(2,1)}), bf16[4,2,16,2,32,256]{5,4,3,2,1,0:T(8,128)(2,1)}, u32[]{:S(2)}, u32[]{:S(2)}) async-start(bf16[4,2,16,2,32,256]{5,4,3,2,1,0:T(8,128)(2,1)} %spectra.3), calls=%async_computation.1 | async-start | bytes 8388608 | tf_op jit(solution)/shard_map/all_to_all | solution.py:288
  99.8 360.0 %all-gather.10.cloned.1.call-start = ((), (), s32[]{:S(2)}) async-start(), calls=%async_computation.3 | async-start | bytes 10485760 | tf_op jit(solution)/shard_map/all_gather | solution.py:292
  226.4 196.7 %all-to-all-start = ((bf16[4,2,16,2,32,256]{5,4,3,2,1,0:T(8,128)(2,1)}), bf16[4,2,16,2,32,256]{5,4,3,2,1,0:T(8,128)(2,1)}, u32[]{:S(2)}, u32[]{:S(2)}) async-start(bf16[4,2,16,2,32,256]{5,4,3,2,1,0:T(8,128)(2,1)} %spectra.2), calls=%async_computation | async-start | bytes 8388608 | tf_op jit(solution)/shard_map/all_to_all | solution.py:288
  231.3 201.3 %copy-start.2 = (f32[2,128,256]{2,1,0:T(8,128)S(1)}, f32[2,128,256]{2,1,0:T(8,128)}, u32[]{:S(2)}) copy-start(f32[2,128,256]{2,1,0:T(8,128)} %get-tuple-element.10) | copy-start | bytes 786436
  231.4 352.7 %all-gather.8.cloned.1.call-start = ((), (), s32[]{:S(2)}) async-start(), calls=%async_computation.2 | async-start | bytes 10485760 | tf_op jit(solution)/shard_map/all_gather | solution.py:292
  584.0 64.5 %copy-start.1 = (bf16[2,16,2,8]{1,3,2,0:T(8,128)(2,1)S(1)}, bf16[2,16,2,8]{1,3,2,0:T(8,128)(2,1)}, u32[]{:S(2)}) copy-start(bf16[2,16,2,8]{1,3,2,0:T(8,128)(2,1)} %param.9) | copy-start | bytes 3076
Sparse Core Ops, SparseCore 0:
  196.2 238.1 all-gather.9
  436.0 148.0 all-gather.7
